TPU v7x, 32 devices: a whole 2x2x4 slice. The times are simulated.
32 devices in a mesh: blk: 8 (over z, y), pix: 4 (over x, core).
Axes of the slice: x: 2, y: 2, z: 4, core: 2. Of those that a mesh axis runs over, the one named last changes fastest.
Arguments:
- pixels: bfloat16 [32768, 224], P(('blk', 'pix')), may hold values from -6 to 6
- bundles: bfloat16 [16, 224, 64], P('blk'), may hold values from -0.375 to 0.375
- assign: int32 [32768, 1], P(('blk', 'pix')), may hold values from 0 to 15; in each aligned block of 1024 rows (0 to 1023, 1024 to 2047, ...) at most 128 rows name the same one
Outputs:
- abundances: float32 [32768, 64], P(('blk', 'pix'))
- residual_energy: float32 [8, 16], P('blk')
Inputs may be any that keep to these rules, and one draw needn't show every extreme that they name: `assign`: among the 1024 rows of one device no bundle is named more than 128 times; in every draw some device names some bundle exactly 128 times; every bundle is named somewhere.
All inputs are finite; a program needn't handle non-finite values. Where the computation divides by a largest or mean magnitude, that divisor is 1e-20 or more.
Results may differ from a plain program's by a relative error of at most 0.0003.
Values may be sent and summed in bfloat16 or wider, within the bound.
A program may use at most 64 MiB of HBM per device.

v0:
```python
import jax
import jax.numpy as jnp
from jax import lax
from jax.sharding import PartitionSpec as P

ITERS = 8
sum_weight = 0.015625


def make_slots(assign, count, cap):
    labels = assign[:, 0]
    onehot = (labels[:, None] == jnp.arange(count, dtype=jnp.int32)[None, :]).astype(jnp.int32)
    ranked = jnp.sum(jnp.cumsum(onehot, axis=0) * onehot, axis=1) - 1
    return labels * cap + ranked


def gram_of(spectra):
    gram = (
        jnp.einsum("nbm,nbk->nmk", spectra, spectra, preferred_element_type=jnp.float32)
        + sum_weight
    )
    step = 1.0 / jnp.max(jnp.sum(jnp.abs(gram), axis=2), axis=1)
    return (gram, step)


def solve(blocks, spectra, gram, step):
    target = (
        jnp.einsum("nsb,nbm->nsm", blocks, spectra, preferred_element_type=jnp.float32) + sum_weight
    )

    def sweep(index, state):
        grad = jnp.einsum("nsm,nmk->nsk", state, gram, precision=lax.Precision.HIGHEST)
        return jnp.maximum(state - step[:, None, None] * (grad - target), 0.0)

    state = lax.fori_loop(0, ITERS, sweep, jnp.zeros_like(target))
    fitted = jnp.einsum(
        "nsm,nbm->nsb", state, spectra.astype(jnp.float32), precision=lax.Precision.HIGHEST
    )
    misfit = blocks.astype(jnp.float32) - fitted
    return (state, jnp.sum(misfit * misfit, axis=-1))


def per_device(pixels, bundles, assign):
    rows, bands = pixels.shape
    width = bundles.shape[2]
    owned = bundles.shape[0]
    count = lax.axis_size("blk") * owned
    cap = 2 * rows // count
    slots = make_slots(assign, count, cap)
    flat = jnp.zeros((count * cap, bands), jnp.bfloat16).at[slots].set(pixels)
    buckets = flat.reshape(count, cap, bands)
    valid = jnp.zeros((count * cap,), jnp.float32).at[slots].set(1.0).reshape(count, cap)
    piece = lax.all_gather(bundles, "blk", axis=0, tiled=True)
    grams, steps = gram_of(piece)
    state, misfit = solve(buckets, piece, grams, steps)
    chosen = state.reshape(count * cap, width)[slots]
    scale = bands * rows * lax.axis_size("pix") / count
    energy = jnp.sum(misfit * valid / scale, axis=1)
    total = lax.psum(energy, "pix")
    return (chosen, total[None, :])


def solution(mesh):
    placed = (P(("blk", "pix"), None), P("blk", None, None), P(("blk", "pix"), None))
    return jax.shard_map(
        per_device,
        mesh=mesh,
        in_specs=placed,
        out_specs=(P(("blk", "pix"), None), P("blk", None)),
        check_vma=False,
    )
```

profile of v0, /device:TPU:0, one launch (start us, length us, event | category | flops | bytes accessed | tf_op | source)
XLA Modules:
  0.0 69.8 jit_solution(9833450703897635159)
XLA Ops:
  0.6 0.0 copy-start
  0.6 0.7 %fusion.11 = s32[16,8,128]{2,1,0:T(8,128)S(1)} fusion(s32[8,128]{1,0:T(8,128)} %bitcast.42), kind=kLoop, calls=%fused_computation.22 | loop fusion | flops 32768 | bytes 69632 | tf_op jit(solution)/shard_map/convert_element_type | solution.py:12
  1.4 4.5 %reduce-window.6 = s32[16,8,128]{2,1,0:T(8,128)S(1)} reduce-window(s32[16,8,128]{2,1,0:T(8,128)S(1)} %fusion.11, s32[]{:T(128)} %constant.5.clone.1), window={size=1x1x128 pad=0_0x0_0x127_0}, to_apply=%region_2.3 | reduce-window | flops 2080768 | bytes 131076 | tf_op jit(solution)/shard_map/reduce-window
  5.9 0.1 slice.10
  6.0 0.1 copy.25
  6.1 0.1 copy.26
  6.2 0.1 broadcast_add_fusion
  6.3 0.7 %fusion.10 = s32[1024]{0:T(1024)S(1)} fusion(s32[2,8,8,128]{3,2,1,0:T(8,128)S(1)} %bitcast.41, s32[1024]{0:T(1024)} %bitcast.43), kind=kLoop, calls=%fused_computation.19 | loop fusion | flops 48128 | bytes 73728 | tf_op jit(solution)/shard_map/reduce_sum | solution.py:13
  7.0 0.7 %compare_select_fusion = s32[1024,1]{0,1:T(1,128)S(1)} fusion(s32[1024,1]{0,1:T(1,128)S(1)} %bitcast.48, s32[1024,1]{0,1:T(1,128)} %param.7), kind=kLoop, calls=%fused_computation.24 | loop fusion | flops 5120 | bytes 12288 | tf_op jit(solution)/shard_map/select_n | solution.py:50
  7.7 4.3 %scatter_custom_fusion.1 = f32[2048]{0:T(1024)S(1)} fusion(s32[1024]{0:T(1024)S(1)} %bitcast.45, f32[1024]{0:T(1024)S(1)} %broadcast.53, f32[]{:T(128)} %constant.17.clone.1), kind=kCustom, calls=%fused_computation.28 | custom fusion | bytes 8196 | tf_op jit(solution)/shard_map/scatter | solution.py:52
  12.1 33.2 %all_gather.3 = bf16[16,224,64]{1,2,0:T(8,128)(2,1)S(1)} all-gather(bf16[2,224,64]{1,2,0:T(8,128)(2,1)} %param.6), channel_id=1, replica_groups=mesh['blk'=8,'pix'=4] {'blk'}, dimensions={0}, use_global_device_ids=true | all-gather | bytes 516096 | tf_op jit(solution)/shard_map/all_gather | solution.py:53
  45.3 0.2 copy.27
  45.5 5.3 %scatter_custom_fusion = bf16[2048,224]{1,0:T(8,128)(2,1)S(1)} fusion(s32[1024]{0:T(1024)S(1)} %bitcast.47, bf16[1024,224]{1,0:T(8,128)(2,1)S(1)} %copy.27, bf16[]{:T(256)} %constant.21.clone.1), kind=kCustom, calls=%fused_computation.14 | custom fusion | bytes 917506 | tf_op jit(solution)/shard_map/scatter | solution.py:50
  50.8 0.5 convolution_add_fusion
  51.3 0.6 copy.29
  51.9 0.3 abs_reduce_fusion
  52.2 0.1 reduce_max.9
  52.4 6.0 %while.11 = (s32[]{:T(128)}, f32[16,128,64]{1,2,0:T(8,128)S(1)}, f32[16]{0:T(128)S(1)}, f32[16,64,64]{1,2,0:T(8,128)S(1)}, f32[16,128,64]{1,2,0:T(8,128)S(1)}, /*index=5*/s32[]{:T(128)}, s32[]{:T(128)}) while((s32[]{:T(128)}, f32[16,128,64]{1,2,0:T(8,128)S(1)}, f32[16]{0:T(128)S(1)}, f32[16,64,64]{1,2,0:T(8,128)S(1)}, ...), condition=%wide.region_7.8_spmd.clone, body=%wide.region_6.7_spmd.clone.sunk | while | flops 101449728 | bytes 2883735 | solution.py:35
  52.4 0.7 fusion.28
  53.2 0.7 fusion.28
  53.9 0.7 fusion.28
  54.7 0.7 fusion.28
  55.4 0.7 fusion.28
  56.2 0.7 fusion.28
  56.9 0.7 fusion.28
  57.7 0.7 fusion.28
  58.4 1.1 %multiply_reduce_fusion = f32[16,128]{1,0:T(8,128)S(1)} fusion(bf16[16,128,224]{1,2,0:T(8,128)(2,1)S(1)} %copy.29, f32[16,128,64]{1,2,0:T(8,128)S(1)} %get-tuple-element.29, bf16[16,224,64]{1,2,0:T(8,128)(2,1)S(1)} %all_gather.3), kind=kOutput, calls=%fused_computation.11 | convolution fusion | flops 354154496 | bytes 1908736 | tf_op jit(solution)/shard_map/nsm,nbm->nsb/dot_general | solution.py:36
  59.5 0.1 fusion.13
  59.6 6.2 %psum.7 = f32[1,16]{1,0:T(1,128)} all-reduce(f32[1,16]{1,0:T(1,128)S(1)} %bitcast.49), channel_id=1, replica_groups=mesh['blk'=8,'pix'=4] {'pix'}, use_global_device_ids=true, to_apply=%region_11.12 | all-reduce | flops 16 | bytes 128 | tf_op jit(solution)/shard_map/psum | solution.py:59
  65.8 0.3 copy.30
  66.1 2.8 %gather_fusion = f32[1024,64]{1,0:T(8,128)S(1)} fusion(f32[2048,64]{1,0:T(8,128)S(1)} %bitcast.38, s32[1024]{0:T(1024)S(1)} %broadcast_clamp_fusion), kind=kCustom, calls=%fused_computation | custom fusion | bytes 528384 | tf_op jit(solution)/shard_map/gather | solution.py:56
  68.9 0.9 %copy.32 = f32[1024,64]{0,1:T(8,128)} copy(f32[1024,64]{1,0:T(8,128)S(1)} %gather_fusion) | data formatting | bytes 524288
  (16 shorter events, 0.3 us)
Async XLA Ops:
  0.6 44.7 %copy-start = (bf16[1024,224]{0,1:T(8,128)(2,1)S(1)}, bf16[1024,224]{0,1:T(8,128)(2,1)}, u32[]{:S(2)}) copy-start(bf16[1024,224]{0,1:T(8,128)(2,1)} %param.5) | copy-start | bytes 1376260
where the time goes:
time: 70.1 us; the launch traced here: 69.8 us
  blocking collectives  39.4 us (56%)
  local copies, waits for them, and re-layouts  15 us (21%)
  matrix products  7.35 us (10%)
  other arithmetic  7.02 us (10%)
  between operations  0.75 us (1%)
    all_gather x1, blocking collectives, per_device(): piece = lax.all_gather(bundles, 'blk', axis=0, tiled=True)  33.2 us
    psum x1, blocking collectives, per_device(): total = lax.psum(energy, 'pix')  6.17 us
    dot_general x8, matrix products, sweep(): jnp.einsum('nsm,nmk->nsk', state, gram, precision=lax.Precision.HIGHEST)  5.45 us
    scatter x1, local copies, waits for them, and re-layouts, per_device(): flat = jnp.zeros((count * cap, bands), jnp.bfloat16).at[slots].set(pixels)  5.28 us
    another operation x3, other arithmetic  4.61 us
    scatter x1, local copies, waits for them, and re-layouts, per_device(): jnp.zeros((count * cap,), jnp.float32).at[slots].set(1.0)  4.32 us
    gather x1, local copies, waits for them, and re-layouts, per_device(): chosen = state.reshape(count * cap, width)[slots]  2.81 us

commit v1 on v0

--- a/solution.py
+++ b/solution.py
@@ -56,7 +56,7 @@
     chosen = state.reshape(count * cap, width)[slots]
     scale = bands * rows * lax.axis_size("pix") / count
     energy = jnp.sum(misfit * valid / scale, axis=1)
-    total = lax.psum(energy, "pix")
+    total = lax.all_gather(energy, axis_name="pix").sum(axis=0)
     return (chosen, total[None, :])
 
 

time: 70.1 us -> 72.3 us (1.031)
  local copies, waits for them, and re-layouts: 15 us -> 16.7 us
    psum x1 -> x0, blocking collectives: 6.17 us -> none  [per_device(): total = lax.psum(energy, 'pix')]
    unnamed x0 -> x1, blocking collectives: none -> 5.63 us
    unnamed x4 -> x7, local copies, waits for them, and re-layouts: 1.1 us -> 2.63 us
where the time goes in v1:
time: 72.3 us; the launch traced here: 72.1 us
  blocking collectives  38.9 us (54%)
  local copies, waits for them, and re-layouts  16.7 us (23%)
  other arithmetic  7.5 us (10%)
  matrix products  7.34 us (10%)
  between operations  1.42 us (2%)
    all_gather x1, blocking collectives, per_device(): piece = lax.all_gather(bundles, 'blk', axis=0, tiled=True)  33.2 us
    unnamed x1, blocking collectives  5.63 us
    dot_general x8, matrix products, sweep(): jnp.einsum('nsm,nmk->nsk', state, gram, precision=lax.Precision.HIGHEST)  5.45 us
    scatter x1, local copies, waits for them, and re-layouts, per_device(): flat = jnp.zeros((count * cap, bands), jnp.bfloat16).at[slots].set(pixels)  5.28 us
    another operation x3, other arithmetic  4.61 us
    scatter x1, local copies, waits for them, and re-layouts, per_device(): jnp.zeros((count * cap,), jnp.float32).at[slots].set(1.0)  4.32 us
    gather x1, local copies, waits for them, and re-layouts, per_device(): chosen = state.reshape(count * cap, width)[slots]  2.81 us
    unnamed x7, local copies, waits for them, and re-layouts  2.63 us

profile of v1, /device:TPU:0, one launch (start us, length us, event | category | flops | bytes accessed | tf_op | source)
XLA Modules:
  0.0 72.1 jit_solution(12030111681565185113)
XLA Ops:
  0.6 1.3 %dynamic-slice = u32[1]{0:T(128)} dynamic-slice(u32[32]{0:T(128)} %constant.40, u32[]{:T(128)S(6)} %add.40), dynamic_slice_sizes={1} | dynamic-slice | bytes 12
  2.6 0.7 fusion.11
  3.3 4.5 %reduce-window.6 = s32[16,8,128]{2,1,0:T(8,128)S(1)} reduce-window(s32[16,8,128]{2,1,0:T(8,128)S(1)} %fusion.11, s32[]{:T(128)} %constant.5.clone.1), window={size=1x1x128 pad=0_0x0_0x127_0}, to_apply=%region_2.3 | reduce-window | flops 2080768 | bytes 131076 | tf_op jit(solution)/shard_map/reduce-window
  7.9 0.1 copy.25
  8.1 0.1 broadcast_add_fusion
  8.2 0.7 fusion.10
  8.9 0.7 compare_select_fusion
  9.6 4.3 %scatter_custom_fusion.1 = f32[2048]{0:T(1024)S(1)} fusion(s32[1024]{0:T(1024)S(1)} %bitcast.46, f32[1024]{0:T(1024)S(1)} %broadcast.53, f32[]{:T(128)} %constant.17.clone.1), kind=kCustom, calls=%fused_computation.28 | custom fusion | bytes 8196 | tf_op jit(solution)/shard_map/scatter | solution.py:52
  14.0 33.2 %all_gather.9 = bf16[16,224,64]{1,2,0:T(8,128)(2,1)S(1)} all-gather(bf16[2,224,64]{1,2,0:T(8,128)(2,1)} %param.6), channel_id=1, replica_groups=mesh['blk'=8,'pix'=4] {'blk'}, dimensions={0}, use_global_device_ids=true | all-gather | bytes 516096 | tf_op jit(solution)/shard_map/all_gather | solution.py:53
  47.2 0.2 copy.27
  47.4 5.3 %scatter_custom_fusion = bf16[2048,224]{1,0:T(8,128)(2,1)S(1)} fusion(s32[1024]{0:T(1024)S(1)} %bitcast.48, bf16[1024,224]{1,0:T(8,128)(2,1)S(1)} %copy.27, bf16[]{:T(256)} %constant.21.clone.1), kind=kCustom, calls=%fused_computation.14 | custom fusion | bytes 917506 | tf_op jit(solution)/shard_map/scatter | solution.py:50
  52.7 0.5 convolution_add_fusion
  53.2 0.6 copy.29
  53.8 0.3 abs_reduce_fusion
  54.1 0.1 reduce_max.9
  54.3 6.0 %while.11 = (s32[]{:T(128)}, f32[16,128,64]{1,2,0:T(8,128)S(1)}, f32[16]{0:T(128)S(1)}, f32[16,64,64]{1,2,0:T(8,128)S(1)}, f32[16,128,64]{1,2,0:T(8,128)S(1)}, /*index=5*/s32[]{:T(128)}, s32[]{:T(128)}) while((s32[]{:T(128)}, f32[16,128,64]{1,2,0:T(8,128)S(1)}, f32[16]{0:T(128)S(1)}, f32[16,64,64]{1,2,0:T(8,128)S(1)}, ...), condition=%wide.region_7.8_spmd.clone, body=%wide.region_6.7_spmd.clone.sunk | while | flops 101449728 | bytes 2883735 | solution.py:35
  54.3 0.7 fusion.28
  55.1 0.7 fusion.28
  55.8 0.7 fusion.28
  56.6 0.7 fusion.28
  57.3 0.7 fusion.28
  58.1 0.7 fusion.28
  58.8 0.7 fusion.28
  59.6 0.7 fusion.28
  60.3 1.1 %multiply_reduce_fusion = f32[16,128]{1,0:T(8,128)S(1)} fusion(bf16[16,128,224]{1,2,0:T(8,128)(2,1)S(1)} %copy.29, f32[16,128,64]{1,2,0:T(8,128)S(1)} %get-tuple-element.29, bf16[16,224,64]{1,2,0:T(8,128)(2,1)S(1)} %all_gather.9), kind=kOutput, calls=%fused_computation.11 | convolution fusion | flops 354154496 | bytes 1908736 | tf_op jit(solution)/shard_map/nsm,nbm->nsb/dot_general | solution.py:36
  61.4 0.1 fusion.13
  61.5 0.2 dynamic-update-slice
  61.8 5.6 %all-reduce = f32[64]{0:T(128)S(1)} all-reduce(f32[64]{0:T(128)S(1)} %dynamic-update-slice), channel_id=2, replica_groups=mesh['blk'=8,'pix'=4] {'pix'}, use_global_device_ids=true, to_apply=%add | all-reduce | flops 64 | bytes 512
  67.5 0.5 reduce_sum.49
  68.0 0.3 copy.30
  68.4 2.8 %gather_fusion = f32[1024,64]{1,0:T(8,128)S(1)} fusion(f32[2048,64]{1,0:T(8,128)S(1)} %bitcast.39, s32[1024]{0:T(1024)S(1)} %broadcast_clamp_fusion), kind=kCustom, calls=%fused_computation | custom fusion | bytes 528384 | tf_op jit(solution)/shard_map/gather | solution.py:56
  71.2 0.9 %copy.32 = f32[1024,64]{0,1:T(8,128)} copy(f32[1024,64]{1,0:T(8,128)S(1)} %gather_fusion) | data formatting | bytes 524288
  (21 shorter events, 0.6 us)
Async XLA Ops:
  0.6 46.6 %copy-start = (bf16[1024,224]{0,1:T(8,128)(2,1)S(1)}, bf16[1024,224]{0,1:T(8,128)(2,1)}, u32[]{:S(2)}) copy-start(bf16[1024,224]{0,1:T(8,128)(2,1)} %param.5) | copy-start | bytes 1376260
